TPU v7x, 32 devices: a whole 2x2x4 slice. The times are simulated.
32 devices in a mesh: bank: 8 (over z, y), ens: 4 (over x, core).
Axes of the slice: x: 2, y: 2, z: 4, core: 2. Of those that a mesh axis runs over, the one named last changes fastest.
Arguments:
- item_ids: int32 [1024, 2], P(('ens', 'bank')), parts along dimension 0, may hold values from 0 to 2047
- large_table: bfloat16 [8192, 256], P(('ens', 'bank')), parts along dimension 0, may hold values from -6 to 6
- dense_part: float32 [1024, 256], P(('ens', 'bank')), parts along dimension 0, may hold values from -6 to 6
- small_ids: int32 [1024], P(('ens', 'bank')), parts along dimension 0, may hold values from 0 to 15
- small_table: bfloat16 [64, 256], P(('ens', 'bank')), parts along dimension 0, may hold values from -6 to 6
- scale_ids: int32 [1024], P(('ens', 'bank')), parts along dimension 0, may hold values from 0 to 15
Outputs:
- features: float32 [1024, 256], P(('ens', 'bank')), parts along dimension 0
There are 4 independent parts, one for each index of `ens`. A program takes and returns all parts, laid end to end along the dimension named above; each array names one. Nothing has to cross between parts.
All inputs are finite; a program needn't handle non-finite values.
Results may differ from a plain program's by a relative error of at most 0.0003.
Values may be sent and summed in bfloat16 or wider, within the bound.
A program may use at most 64 MiB of HBM per device.

v0:
```python
import jax
import jax.numpy as jnp
from jax import lax
from jax.sharding import PartitionSpec as P

PICKS = 2


def local_rows(table_part, wanted, first_row):
    place = wanted - first_row
    inside = (place >= 0) & (place < table_part.shape[0])
    found = jnp.take(table_part, jnp.clip(place, 0, table_part.shape[0] - 1), axis=0).astype(
        jnp.float32
    )
    return jnp.where(inside[..., None], found, 0.0)


def shards(item_ids, large_table, dense_part, small_ids, small_table, scale_ids):
    big_first = lax.axis_index("bank") * large_table.shape[0]
    all_ids = lax.all_gather(item_ids, "bank", axis=0, tiled=True)
    pooled = lax.psum_scatter(
        jnp.sum(local_rows(large_table, all_ids, big_first), axis=1),
        "bank",
        scatter_dimension=0,
        tiled=True,
    ) * PICKS ** (-0.5)
    every_row = lax.all_gather(small_table, "bank", axis=0, tiled=True)
    small_rows = jnp.take(every_row, small_ids, axis=0).astype(jnp.float32)
    scale_rows = jnp.take(every_row, scale_ids, axis=0).astype(jnp.float32)
    dense_part = dense_part * scale_rows
    total = dense_part + pooled * small_rows
    power = jnp.mean(total * total, axis=-1, keepdims=True)
    features = total * lax.rsqrt(power + 1e-06)
    return features


def solution(mesh):
    return jax.shard_map(
        shards,
        mesh=mesh,
        in_specs=(
            P(("ens", "bank"), None),
            P(("ens", "bank"), None),
            P(("ens", "bank"), None),
            P(("ens", "bank")),
            P(("ens", "bank"), None),
            P(("ens", "bank")),
        ),
        out_specs=P(("ens", "bank"), None),
        check_vma=False,
    )
```

profile of v0, /device:TPU:0, one launch (start us, length us, event | category | flops | bytes accessed | tf_op | source)
XLA Modules:
  0.0 102.9 jit_solution(7477630568052057338)
XLA Ops:
  6.5 0.0 copy-start
  6.5 0.0 reduce-scatter.2.cloned.1.call-start
  6.5 0.0 copy-start.2
  6.5 0.7 copy-done.2
  7.3 22.3 %all-gather.1 = s32[8,32,2]{1,2,0:T(2,128)S(1)} all-gather(s32[1,32,2]{1,2,0:T(2,128)S(1)} %bitcast.6), channel_id=1, replica_groups=mesh['bank'=8,'ens'=4] {'bank'}, dimensions={0}, use_global_device_ids=true | all-gather | bytes 2304 | tf_op jit(solution)/shard_map/all_gather | solution.py:20
  29.6 0.1 reshape.59
  29.7 0.1 copy.20
  29.8 0.1 reshape.37
  30.0 0.0 copy-done
  30.0 2.0 %gather_fusion = bf16[512,256]{1,0:T(8,128)(2,1)S(1)} fusion(bf16[256,256]{1,0:T(8,128)(2,1)S(1)} %copy-done, s32[1024]{0:T(1024)S(1)} %pad_clamp_fusion.1), kind=kCustom, calls=%fused_computation.2 | custom fusion | bytes 526336 | tf_op jit(solution)/shard_map/jit(_take)/gather | solution.py:12
  31.9 0.1 reshape.36
  32.1 0.2 copy.19
  32.2 0.2 copy.21
  32.4 2.4 %select_reduce_fusion = f32[256,256]{1,0:T(8,128)} fusion(pred[256,2]{1,0:T(8,128)(4,1)S(1)} %bitcast.5, bf16[256,2,256]{2,1,0:T(2,128)(2,1)S(1)} %reshape.36, pred[256,2]{1,0:T(8,128)(4,1)S(1)} %copy.19), kind=kLoop, calls=%fused_computation.3 | loop fusion | flops 458752 | bytes 525312 | tf_op jit(solution)/shard_map/reduce_sum | solution.py:22
  34.8 0.0 reduce-scatter.2.cloned.1.call-update
  34.9 0.0 copy-start.3
  34.9 0.7 copy-done.3
  35.5 16.3 %all-gather = bf16[8,2,256]{2,1,0:T(2,128)(2,1)S(1)} all-gather(bf16[1,2,256]{2,1,0:T(2,128)(2,1)S(1)} %bitcast.7), channel_id=1, replica_groups=mesh['bank'=8,'ens'=4] {'bank'}, dimensions={0}, use_global_device_ids=true | all-gather | bytes 9216 | tf_op jit(solution)/shard_map/all_gather | solution.py:27
  51.8 0.0 copy-start.5
  51.8 0.6 copy-done.5
  52.5 0.0 copy-start.4
  52.5 0.6 gather_fusion.1
  53.1 0.0 copy-done.4
  53.2 0.0 copy-start.1
  53.2 0.6 gather_fusion.2
  53.8 40.6 %reduce-scatter.2.cloned.1.call-done = f32[32,256]{1,0:T(8,128)} async-done(((f32[256,256]{1,0:T(8,128)}), f32[32,256]{1,0:T(8,128)}) %reduce-scatter.2.cloned.1.call-update) | async-done | bytes 32784 | tf_op jit(solution)/shard_map/reduce_scatter | solution.py:21
  94.4 0.0 copy-done.1
  94.4 0.9 multiply_reduce_fusion
  95.3 0.7 broadcast_multiply_fusion
  (12 shorter events, 0.1 us)
Async XLA Ops:
  6.5 23.4 %copy-start = (bf16[256,256]{1,0:T(8,128)(2,1)S(1)}, bf16[256,256]{1,0:T(8,128)(2,1)}, u32[]{:S(2)}) copy-start(bf16[256,256]{1,0:T(8,128)(2,1)} %param.9) | copy-start | bytes 393220
  6.5 87.8 %reduce-scatter.2.cloned.1.call-start = ((), (), s32[]{:S(2)}) async-start(), calls=%async_computation.1 | async-start | bytes 294912 | tf_op jit(solution)/shard_map/reduce_scatter | solution.py:21
  6.5 0.7 copy-start.2
  34.9 0.7 copy-start.3
  51.8 0.7 copy-start.5
  52.5 0.7 copy-start.4
  53.2 41.2 %copy-start.1 = (f32[32,256]{1,0:T(8,128)S(1)}, f32[32,256]{1,0:T(8,128)}, u32[]{:S(2)}) copy-start(f32[32,256]{1,0:T(8,128)} %param.10) | copy-start | bytes 98308
Sparse Core Ops, SparseCore 0:
  35.0 59.3 reduce-scatter.1
where the time goes:
time: 103 us
  waiting for transfers between devices  40.6 us (39%)
  blocking collectives  38.6 us (37%)
  between operations  13.5 us (13%)
  local copies, waits for them, and re-layouts  6.08 us (6%)
  other arithmetic  4.16 us (4%)
    reduce_scatter x1, waiting for transfers between devices, shards(): lax.psum_scatter(jnp.sum(local_rows(large_table, all_ids, big_first), axi...  40.6 us
    all_gather x1, blocking collectives, shards(): all_ids = lax.all_gather(item_ids, 'bank', axis=0, tiled=True)  22.3 us
    all_gather x1, blocking collectives, shards(): every_row = lax.all_gather(small_table, 'bank', axis=0, tiled=True)  16.3 us
    reduce_sum x1, other arithmetic, shards(): jnp.sum(local_rows(large_table, all_ids, big_first), axis=1)  2.44 us
    unnamed x13, local copies, waits for them, and re-layouts  2.07 us
  transfers between devices with their start and end apart: 1, of which 1 were waited for; matrix products, arithmetic and copies ran while one was open for 1% of the time, Pallas kernels for 0%

commit v1 on v0

v1 whole, which is shorter than its diff:
```python
import functools

import jax
import jax.numpy as jnp
from jax import lax
from jax.experimental import pallas as pl
from jax.experimental.pallas import tpu as pltpu
from jax.sharding import PartitionSpec as P

MESH = pl.DeviceIdType.MESH
PICKS = 2
CHUNKS = 2


def column(row, eye):
    wide = jnp.where(eye, row.astype(jnp.float32), 0.0)
    return jnp.sum(wide, axis=1, keepdims=True)


def kernel(n, ids_in, tab_in, dense_in, sid_in, small_in, cid_in, out, ids, tab, dense, sid, small, cid, part, got,
           lsem, tsem, ids_s, ids_r, tab_s, tab_r, sp_s, sp_r, sl_s, sl_r, part_s, part_r):
    line = n // 2
    me = lax.axis_index("bank")
    z, y = lax.div(me, 2), lax.rem(me, 2)
    partner = me + 1 - 2 * y
    rows, feats = tab_in.shape
    examples = dense_in.shape[0]
    width = feats // CHUNKS

    def on_line(d):
        return lax.rem(z + line + d, line) * 2 + y

    def cols(c):
        return pl.ds(c * width, width)

    local = [
        pltpu.make_async_copy(ids_in, ids.at[0], lsem.at[0]),
        pltpu.make_async_copy(small_in, small.at[z, y], lsem.at[1]),
        pltpu.make_async_copy(sid_in, sid, lsem.at[2]),
        pltpu.make_async_copy(cid_in, cid, lsem.at[3]),
        pltpu.make_async_copy(dense_in, dense, lsem.at[4]),
    ]
    tables = [
        pltpu.make_async_copy(tab_in.at[:, cols(c)], tab.at[0, c], tsem.at[c]) for c in range(CHUNKS)
    ]
    for copy in local[:2] + tables + local[2:]:
        copy.start()

    barrier = pltpu.get_barrier_semaphore()
    for other in [on_line(d) for d in range(1, line)] + [partner]:
        pl.semaphore_signal(barrier, inc=1, device_id={"bank": other}, device_id_type=MESH)
    pl.semaphore_wait(barrier, line)

    def remote(src, dst, send, recv, other):
        return pltpu.make_async_remote_copy(
            src_ref=src, dst_ref=dst, send_sem=send, recv_sem=recv, device_id={"bank": other}, device_id_type=MESH
        )

    sends = []
    local[0].wait()
    id_copies = [remote(ids.at[0], ids.at[d], ids_s.at[d], ids_r.at[d], on_line(d)) for d in range(1, line)]
    for copy in id_copies:
        copy.start()
    tab_copies = []
    for c in range(CHUNKS):
        tables[c].wait()
        copy = remote(tab.at[0, c], tab.at[1, c], tab_s.at[c], tab_r.at[c], partner)
        copy.start()
        tab_copies.append(copy)
        if c == 0:
            local[1].wait()
            small_pair = remote(small.at[z, y], small.at[z, y], sp_s.at[0], sp_r.at[0], partner)
            small_pair.start()
    for copy in local[2:]:
        copy.wait()

    eye = lax.broadcasted_iota(jnp.int32, (examples, examples), 0) == lax.broadcasted_iota(
        jnp.int32, (examples, examples), 1
    )
    lanes = lax.broadcasted_iota(jnp.int32, (1, rows), 1).astype(jnp.float32)
    first = [(owner * rows).astype(jnp.float32) for owner in (me, partner)]

    for copy in id_copies:
        copy.wait_recv()
    counts = [[], []]
    for d in range(line):
        picks = [column(ids[d, p : p + 1, :], eye) for p in range(PICKS)]
        for side in range(2):
            at = lanes + first[side]
            counts[side].append(sum(jnp.where(pick == at, 1.0, 0.0) for pick in picks))
    counts = [jnp.concatenate(c, axis=0).astype(jnp.bfloat16) for c in counts]

    part_copies = []
    kept = []
    for c in range(CHUNKS):
        mine = jnp.dot(counts[0], tab[0, c], preferred_element_type=jnp.float32)
        tab_copies[c].wait_recv()
        both = mine + jnp.dot(counts[1], tab[1, c], preferred_element_type=jnp.float32)
        part[c] = both
        for d in range(1, line):
            copy = remote(
                part.at[c, pl.ds(d * examples, examples)], got.at[c, d], part_s.at[c, d], part_r.at[c, d], on_line(-d)
            )
            copy.start()
            part_copies.append(copy)
        if c == 0:
            small_pair.wait_recv()
            small_line = [remote(small.at[z], small.at[z], sl_s.at[d], sl_r.at[d], on_line(d)) for d in range(1, line)]
            for copy in small_line:
                copy.start()

    for copy in small_line:
        copy.wait_recv()
    small_id, scale_id = column(sid[...], eye), column(cid[...], eye)
    small_rows = jnp.zeros((examples, feats), jnp.float32)
    scale_rows = jnp.zeros((examples, feats), jnp.float32)
    held = small_in.shape[0]
    for b in range(n):
        block = small[b // 2, b % 2].astype(jnp.float32)
        for r in range(held):
            row = block[r : r + 1, :]
            small_rows = jnp.where(small_id == float(b * held + r), row, small_rows)
            scale_rows = jnp.where(scale_id == float(b * held + r), row, scale_rows)
    base = dense[...] * scale_rows

    totals = []
    for c in range(CHUNKS):
        pooled = part[c, :examples]
        for d in range(1, line):
            part_copies[c * (line - 1) + d - 1].wait_recv()
            pooled = pooled + got[c, d]
        span = slice(c * width, (c + 1) * width)
        totals.append(base[:, span] + pooled * PICKS ** (-0.5) * small_rows[:, span])
    power = sum(jnp.sum(t * t, axis=1, keepdims=True) for t in totals) * (1.0 / feats)
    scale = lax.rsqrt(power + 1e-06)
    for c in range(CHUNKS):
        out[:, cols(c)] = totals[c] * scale
    for copy in id_copies + tab_copies + [small_pair] + small_line + part_copies:
        copy.wait_send()


def solution(mesh):
    n = mesh.shape["bank"]
    line = n // 2

    def shards(item_ids, large_table, dense_part, small_ids, small_table, scale_ids):
        rows, feats = large_table.shape
        examples = dense_part.shape[0]
        held = small_table.shape[0]
        width = feats // CHUNKS
        dma = pltpu.SemaphoreType.DMA
        return pl.pallas_call(
            functools.partial(kernel, n),
            out_shape=jax.ShapeDtypeStruct((examples, feats), jnp.float32),
            in_specs=[pl.BlockSpec(memory_space=pl.ANY)] * 6,
            out_specs=pl.BlockSpec(memory_space=pltpu.VMEM),
            scratch_shapes=[
                pltpu.VMEM((line, PICKS, examples), jnp.int32),
                pltpu.VMEM((2, CHUNKS, rows, width), jnp.bfloat16),
                pltpu.VMEM((examples, feats), jnp.float32),
                pltpu.VMEM((1, examples), jnp.int32),
                pltpu.VMEM((line, 2, held, feats), jnp.bfloat16),
                pltpu.VMEM((1, examples), jnp.int32),
                pltpu.VMEM((CHUNKS, line * examples, width), jnp.float32),
                pltpu.VMEM((CHUNKS, line, examples, width), jnp.float32),
                dma((5,)),
                dma((CHUNKS,)),
                dma((line,)),
                dma((line,)),
                dma((CHUNKS,)),
                dma((CHUNKS,)),
                dma((1,)),
                dma((1,)),
                dma((line,)),
                dma((line,)),
                dma((CHUNKS, line)),
                dma((CHUNKS, line)),
            ],
            compiler_params=pltpu.CompilerParams(collective_id=0, has_side_effects=True),
        )(
            item_ids.T,
            large_table,
            dense_part,
            small_ids.reshape(1, -1),
            small_table,
            scale_ids.reshape(1, -1),
        )

    return jax.shard_map(
        shards,
        mesh=mesh,
        in_specs=(
            P(("ens", "bank"), None),
            P(("ens", "bank"), None),
            P(("ens", "bank"), None),
            P(("ens", "bank")),
            P(("ens", "bank"), None),
            P(("ens", "bank")),
        ),
        out_specs=P(("ens", "bank"), None),
        check_vma=False,
    )
```

time: 103 us -> 16.1 us (0.16)
  waiting for transfers between devices: 40.6 us -> 0 us
  blocking collectives: 38.6 us -> 0 us
  Pallas kernels: 0 us -> 14.6 us
  between operations: 13.5 us -> 0.01 us
  local copies, waits for them, and re-layouts: 6.08 us -> 1.38 us
  other arithmetic: 4.16 us -> 0 us
    reduce_scatter x1 -> x0, waiting for transfers between devices: 40.6 us -> none  [shards(): lax.psum_scatter(jnp.sum(local_rows(large_table, all_ids, big_first), axi...]
    all_gather x2 -> x0, blocking collectives: 38.6 us -> none  [the longest x1 22.3 us: shards(): all_ids = lax.all_gather(item_ids, 'bank', axis=0, tiled=True)]
    pallas_call x0 -> x1, Pallas kernels: none -> 14.6 us  [shards(): pl.pallas_call(functools.partial(kernel, n), out_shape=jax.ShapeDtypeStru...]
    reduce_sum x2 -> x0, other arithmetic: 3.38 us -> none  [the longest x1 2.44 us: shards(): jnp.sum(local_rows(large_table, all_ids, big_first), axis=1)]
    gather x4 -> x0, local copies, waits for them, and re-layouts: 3.31 us -> none  [the longest x2 2.06 us: local_rows(): jnp.take(table_part, jnp.clip(place, 0, table_part.shape[0] - 1), axis=0)]
    unnamed x13 -> x1, local copies, waits for them, and re-layouts: 2.07 us -> 1.38 us
  transfers between devices with their start and end apart: 1 -> 0, of which waited for: 1 -> 0; matrix products, arithmetic and copies ran while one was open for 1% -> 0% of each run, Pallas kernels for 0% -> 0%
where the time goes in v1:
time: 16.1 us; the launch traced here: 15.9 us
  Pallas kernels  14.6 us (91%)
  local copies, waits for them, and re-layouts  1.38 us (9%)
    pallas_call x1, Pallas kernels, shards(): pl.pallas_call(functools.partial(kernel, n), out_shape=jax.ShapeDtypeStru...  14.6 us
    unnamed x1, local copies, waits for them, and re-layouts  1.38 us

profile of v1, /device:TPU:0, one launch (start us, length us, event | category | flops | bytes accessed | tf_op | source)
XLA Modules:
  0.0 15.9 jit_solution(3402114760922494580)
XLA Ops:
  0.0 14.6 %shard_map.64 = f32[32,256]{1,0:T(8,128)} custom-call(s32[2,32]{1,0:T(2,128)} %bitcast.3, bf16[256,256]{1,0:T(8,128)(2,1)} %tab_in.1, f32[32,256]{1,0:T(8,128)} %dense_in.1, s32[1,32]{1,0:T(1,128)} %bitcast.4, bf16[2,256]{1,0:T(2,128)(2,1)} %small_in.1, s32[1,32]{1,0:T(1,128)} %bitcast.5), custom_call_target="tpu_custom_call" | custom-call | tf_op jit(solution)/shard_map/pallas_call | solution.py:152
  14.6 1.4 %copy.8 = f32[32,256]{1,0:T(8,128)} copy(f32[32,256]{1,0:T(8,128)} %shard_map.64) | data formatting | bytes 65536

commit v2 on v1

--- a/solution.py
+++ b/solution.py
@@ -27,14 +27,21 @@
     examples = dense_in.shape[0]
     width = feats // CHUNKS
 
+    sign = 1 - 2 * lax.div(2 * z, line)
+
+    def spot(d):
+        return lax.rem(z + line + sign * d, line)
+
     def on_line(d):
-        return lax.rem(z + line + d, line) * 2 + y
+        return spot(d) * 2 + y
+
+    away = range(line - 1, 0, -1)
 
     def cols(c):
         return pl.ds(c * width, width)
 
     local = [
-        pltpu.make_async_copy(ids_in, ids.at[0], lsem.at[0]),
+        pltpu.make_async_copy(ids_in, ids.at[z], lsem.at[0]),
         pltpu.make_async_copy(small_in, small.at[z, y], lsem.at[1]),
         pltpu.make_async_copy(sid_in, sid, lsem.at[2]),
         pltpu.make_async_copy(cid_in, cid, lsem.at[3]),
@@ -47,7 +54,7 @@
         copy.start()
 
     barrier = pltpu.get_barrier_semaphore()
-    for other in [on_line(d) for d in range(1, line)] + [partner]:
+    for other in [on_line(d) for d in away] + [partner]:
         pl.semaphore_signal(barrier, inc=1, device_id={"bank": other}, device_id_type=MESH)
     pl.semaphore_wait(barrier, line)
 
@@ -56,9 +63,11 @@
             src_ref=src, dst_ref=dst, send_sem=send, recv_sem=recv, device_id={"bank": other}, device_id_type=MESH
         )
 
-    sends = []
+    def landed(ref, recv):
+        remote(ref, ref, ids_s.at[0], recv, partner).wait_recv()
+
     local[0].wait()
-    id_copies = [remote(ids.at[0], ids.at[d], ids_s.at[d], ids_r.at[d], on_line(d)) for d in range(1, line)]
+    id_copies = [remote(ids.at[z], ids.at[z], ids_s.at[d], ids_r.at[z], on_line(d)) for d in away]
     for copy in id_copies:
         copy.start()
     tab_copies = []
@@ -80,8 +89,8 @@
     lanes = lax.broadcasted_iota(jnp.int32, (1, rows), 1).astype(jnp.float32)
     first = [(owner * rows).astype(jnp.float32) for owner in (me, partner)]
 
-    for copy in id_copies:
-        copy.wait_recv()
+    for d in away:
+        landed(ids.at[spot(d)], ids_r.at[spot(d)])
     counts = [[], []]
     for d in range(line):
         picks = [column(ids[d, p : p + 1, :], eye) for p in range(PICKS)]
@@ -97,20 +106,19 @@
         tab_copies[c].wait_recv()
         both = mine + jnp.dot(counts[1], tab[1, c], preferred_element_type=jnp.float32)
         part[c] = both
-        for d in range(1, line):
-            copy = remote(
-                part.at[c, pl.ds(d * examples, examples)], got.at[c, d], part_s.at[c, d], part_r.at[c, d], on_line(-d)
-            )
+        for d in away:
+            share = pl.ds(pl.multiple_of(spot(d) * examples, examples), examples)
+            copy = remote(part.at[c, share], got.at[c, z], part_s.at[c, d], part_r.at[c, z], on_line(d))
             copy.start()
             part_copies.append(copy)
         if c == 0:
             small_pair.wait_recv()
-            small_line = [remote(small.at[z], small.at[z], sl_s.at[d], sl_r.at[d], on_line(d)) for d in range(1, line)]
+            small_line = [remote(small.at[z], small.at[z], sl_s.at[d], sl_r.at[z], on_line(d)) for d in away]
             for copy in small_line:
                 copy.start()
 
-    for copy in small_line:
-        copy.wait_recv()
+    for d in away:
+        landed(small.at[spot(d)], sl_r.at[spot(d)])
     small_id, scale_id = column(sid[...], eye), column(cid[...], eye)
     small_rows = jnp.zeros((examples, feats), jnp.float32)
     scale_rows = jnp.zeros((examples, feats), jnp.float32)
@@ -125,10 +133,10 @@
 
     totals = []
     for c in range(CHUNKS):
-        pooled = part[c, :examples]
+        pooled = part[c, pl.ds(pl.multiple_of(z * examples, examples), examples)]
         for d in range(1, line):
-            part_copies[c * (line - 1) + d - 1].wait_recv()
-            pooled = pooled + got[c, d]
+            landed(got.at[c, spot(d)], part_r.at[c, spot(d)])
+            pooled = pooled + got[c, spot(d)]
         span = slice(c * width, (c + 1) * width)
         totals.append(base[:, span] + pooled * PICKS ** (-0.5) * small_rows[:, span])
     power = sum(jnp.sum(t * t, axis=1, keepdims=True) for t in totals) * (1.0 / feats)
@@ -151,8 +159,8 @@
         dma = pltpu.SemaphoreType.DMA
         return pl.pallas_call(
             functools.partial(kernel, n),
-            out_shape=jax.ShapeDtypeStruct((examples, feats), jnp.float32),
-            in_specs=[pl.BlockSpec(memory_space=pl.ANY)] * 6,
+            out_shape=pltpu.VMEM((examples, feats), jnp.float32),
+            in_specs=[pl.BlockSpec(memory_space=pltpu.HBM)] * 6,
             out_specs=pl.BlockSpec(memory_space=pltpu.VMEM),
             scratch_shapes=[
                 pltpu.VMEM((line, PICKS, examples), jnp.int32),
@@ -176,7 +184,9 @@
                 dma((CHUNKS, line)),
                 dma((CHUNKS, line)),
             ],
-            compiler_params=pltpu.CompilerParams(collective_id=0, has_side_effects=True),
+            compiler_params=pltpu.CompilerParams(
+                collective_id=0, has_side_effects=True
+            ),
         )(
             item_ids.T,
             large_table,

time: 16.1 us -> 14.4 us (0.89)
  Pallas kernels: 14.6 us -> 13.6 us
  local copies, waits for them, and re-layouts: 1.38 us -> 0.62 us
    pallas_call x1, Pallas kernels: 14.6 us -> 13.6 us  [shards(): pl.pallas_call(functools.partial(kernel, n), out_shape=pltpu.VMEM((exampl...]
    unnamed x1, local copies, waits for them, and re-layouts: 1.38 us -> 0.62 us
where the time goes in v2:
time: 14.4 us; the launch traced here: 14.2 us
  Pallas kernels  13.6 us (94%)
  local copies, waits for them, and re-layouts  0.62 us (4%)
    pallas_call x1, Pallas kernels, shards(): pl.pallas_call(functools.partial(kernel, n), out_shape=pltpu.VMEM((exampl...  13.6 us
    unnamed x1, local copies, waits for them, and re-layouts  0.62 us

profile of v2, /device:TPU:0, one launch (start us, length us, event | category | flops | bytes accessed | tf_op | source)
XLA Modules:
  0.0 14.2 jit_solution(13014665893096503198)
XLA Ops:
  0.0 13.6 %shard_map.64 = f32[32,256]{1,0:T(8,128)S(1)} custom-call(s32[2,32]{1,0:T(2,128)} %bitcast.3, bf16[256,256]{1,0:T(8,128)(2,1)} %tab_in.1, f32[32,256]{1,0:T(8,128)} %dense_in.1, s32[1,32]{1,0:T(1,128)} %bitcast.4, bf16[2,256]{1,0:T(2,128)(2,1)} %small_in.1, s32[1,32]{1,0:T(1,128)} %bitcast.5), custom_call_target="tpu_custom_call" | custom-call | tf_op jit(solution)/shard_map/pallas_call | solution.py:160
  13.6 0.6 %copy.8 = f32[32,256]{1,0:T(8,128)} copy(f32[32,256]{1,0:T(8,128)S(1)} %shard_map.64) | data formatting | bytes 65536

commit v3 on v2

--- a/solution.py
+++ b/solution.py
@@ -17,8 +17,8 @@
     return jnp.sum(wide, axis=1, keepdims=True)
 
 
-def kernel(n, ids_in, tab_in, dense_in, sid_in, small_in, cid_in, out, ids, tab, dense, sid, small, cid, part, got,
-           lsem, tsem, ids_s, ids_r, tab_s, tab_r, sp_s, sp_r, sl_s, sl_r, part_s, part_r):
+def kernel(n, ids_in, tab_in, dense_in, sid_in, small_in, cid_in, out, ids, tab, dense, sid, small, cid, part, got, raw,
+           lsem, tsem, ids_s, ids_r, tab_s, tab_r, sp_s, sp_r, sl_s, sl_r, part_s, part_r, raw_s, raw_r, near, here):
     line = n // 2
     me = lax.axis_index("bank")
     z, y = lax.div(me, 2), lax.rem(me, 2)
@@ -53,10 +53,38 @@
     for copy in local[:2] + tables + local[2:]:
         copy.start()
 
+    pusher = me >= n - 2
+    head, tail, corner = me == 0, me == n - 2, me == n - 1
+
+    def unless(condition, is_far, action):
+        if is_far:
+            pl.when(jnp.logical_not(condition))(action)
+        else:
+            action()
+
     barrier = pltpu.get_barrier_semaphore()
-    for other in [on_line(d) for d in away] + [partner]:
+
+    def greet(other):
         pl.semaphore_signal(barrier, inc=1, device_id={"bank": other}, device_id_type=MESH)
-    pl.semaphore_wait(barrier, line)
+
+    @pl.when(head)
+    def _():
+        greet(n - 1)
+
+    for d in away:
+        pl.when(spot(d) > z)(lambda d=d: greet(on_line(d)))
+    pl.when(y == 0)(lambda: greet(partner))
+    pl.when(me > 0)(lambda: pl.semaphore_wait(barrier, z + y + corner.astype(jnp.int32)))
+
+    def answer(sem, other):
+        pl.semaphore_signal(sem, inc=1, device_id={"bank": other}, device_id_type=MESH)
+
+    for d in away:
+        pl.when(spot(d) < z)(lambda d=d: answer(here.at[z], on_line(d)))
+    pl.when(y == 1)(lambda: answer(near, partner))
+
+    def hear(d):
+        pl.when(spot(d) > z)(lambda: pl.semaphore_wait(here.at[spot(d)], 1))
 
     def remote(src, dst, send, recv, other):
         return pltpu.make_async_remote_copy(
@@ -67,19 +95,41 @@
         remote(ref, ref, ids_s.at[0], recv, partner).wait_recv()
 
     local[0].wait()
-    id_copies = [remote(ids.at[z], ids.at[z], ids_s.at[d], ids_r.at[z], on_line(d)) for d in away]
-    for copy in id_copies:
-        copy.start()
-    tab_copies = []
+    id_copies = {d: remote(ids.at[z], ids.at[z], ids_s.at[d], ids_r.at[z], on_line(d)) for d in away}
+    for d in away:
+        pl.when(spot(d) < z)(id_copies[d].start)
     for c in range(CHUNKS):
         tables[c].wait()
-        copy = remote(tab.at[0, c], tab.at[1, c], tab_s.at[c], tab_r.at[c], partner)
-        copy.start()
-        tab_copies.append(copy)
-        if c == 0:
-            local[1].wait()
-            small_pair = remote(small.at[z, y], small.at[z, y], sp_s.at[0], sp_r.at[0], partner)
-            small_pair.start()
+    raw_copies = [remote(tab.at[0, c], raw.at[y, c], raw_s.at[c], raw_r.at[y, c], 0) for c in range(CHUNKS)]
+    tab_copies = [remote(tab.at[0, c], tab.at[1, c], tab_s.at[c], tab_r.at[c], partner) for c in range(CHUNKS)]
+    local[1].wait()
+    small_pair = remote(small.at[z, y], small.at[z, y], sp_s.at[0], sp_r.at[0], partner)
+
+    def start_pair():
+        for copy in [small_pair] + tab_copies:
+            copy.start()
+
+    pl.when(y == 1)(start_pair)
+
+    @pl.when(pusher)
+    def _():
+        for copy in raw_copies:
+            copy.start()
+
+    def send_ids(d):
+        hear(d)
+        pl.when(spot(d) > z)(id_copies[d].start)
+
+    if line > 1:
+        unless(head, line == 2, lambda: send_ids(1))
+
+    @pl.when(y == 0)
+    def _():
+        pl.semaphore_wait(near, 1)
+        start_pair()
+
+    for d in range(2, line):
+        unless(head, d == line - 1, lambda d=d: send_ids(d))
     for copy in local[2:]:
         copy.wait()
 
@@ -89,33 +139,40 @@
     lanes = lax.broadcasted_iota(jnp.int32, (1, rows), 1).astype(jnp.float32)
     first = [(owner * rows).astype(jnp.float32) for owner in (me, partner)]
 
-    for d in away:
-        landed(ids.at[spot(d)], ids_r.at[spot(d)])
-    counts = [[], []]
-    for d in range(line):
-        picks = [column(ids[d, p : p + 1, :], eye) for p in range(PICKS)]
-        for side in range(2):
-            at = lanes + first[side]
-            counts[side].append(sum(jnp.where(pick == at, 1.0, 0.0) for pick in picks))
-    counts = [jnp.concatenate(c, axis=0).astype(jnp.bfloat16) for c in counts]
-
+    def counted(spot_of):
+        picks = [column(ids[spot_of, p : p + 1, :], eye) for p in range(PICKS)]
+        return [sum(jnp.where(pick == lanes + f, 1.0, 0.0) for pick in picks).astype(jnp.bfloat16) for f in first]
+
+    def summed(counts, c):
+        return sum(jnp.dot(counts[side], tab[side, c], preferred_element_type=jnp.float32) for side in range(2))
+
+    small_line = {d: remote(small.at[z], small.at[z], sl_s.at[d], sl_r.at[z], on_line(d)) for d in away}
+    small_pair.wait_recv()
+    for d in away:
+        unless(head, d == line - 1, small_line[d].start)
     part_copies = []
-    kept = []
-    for c in range(CHUNKS):
-        mine = jnp.dot(counts[0], tab[0, c], preferred_element_type=jnp.float32)
-        tab_copies[c].wait_recv()
-        both = mine + jnp.dot(counts[1], tab[1, c], preferred_element_type=jnp.float32)
-        part[c] = both
-        for d in away:
-            share = pl.ds(pl.multiple_of(spot(d) * examples, examples), examples)
-            copy = remote(part.at[c, share], got.at[c, z], part_s.at[c, d], part_r.at[c, z], on_line(d))
-            copy.start()
-            part_copies.append(copy)
-        if c == 0:
-            small_pair.wait_recv()
-            small_line = [remote(small.at[z], small.at[z], sl_s.at[d], sl_r.at[z], on_line(d)) for d in away]
-            for copy in small_line:
-                copy.start()
+    for d in range(1, line):
+        unless(tail, d == line - 1, lambda d=d: landed(ids.at[spot(d)], ids_r.at[spot(d)]))
+        if d == line - 1:
+
+            @pl.when(head)
+            def _():
+                pl.semaphore_wait(here.at[spot(line - 1)], 1)
+
+        counts = counted(spot(d))
+        for c in range(CHUNKS):
+            if d == 1:
+                tab_copies[c].wait_recv()
+            part[c, d] = summed(counts, c)
+            copy = remote(part.at[c, d], got.at[c, z], part_s.at[c, d], part_r.at[c, z], on_line(d))
+            unless(tail, d == line - 1, copy.start)
+            part_copies.append((d, copy))
+    pl.when(head)(small_line[line - 1].start)
+    if line == 1:
+        for copy in tab_copies:
+            copy.wait_recv()
+    counts = counted(z)
+    kept = [summed(counts, c) for c in range(CHUNKS)]
 
     for d in away:
         landed(small.at[spot(d)], sl_r.at[spot(d)])
@@ -131,11 +188,23 @@
             scale_rows = jnp.where(scale_id == float(b * held + r), row, scale_rows)
     base = dense[...] * scale_rows
 
+    @pl.when(head)
+    def _():
+        own_picks = [column(ids[z, p : p + 1, :], eye) for p in range(PICKS)]
+        at = [lanes + float((n - 2 + side) * rows) for side in range(2)]
+        for c in range(CHUNKS):
+            far = jnp.zeros((examples, width), jnp.float32)
+            for side in range(2):
+                landed(raw.at[side, c], raw_r.at[side, c])
+                count = sum(jnp.where(pick == at[side], 1.0, 0.0) for pick in own_picks).astype(jnp.bfloat16)
+                far = far + jnp.dot(count, raw[side, c], preferred_element_type=jnp.float32)
+            got[c, line - 1] = far
+
     totals = []
     for c in range(CHUNKS):
-        pooled = part[c, pl.ds(pl.multiple_of(z * examples, examples), examples)]
+        pooled = kept[c]
         for d in range(1, line):
-            landed(got.at[c, spot(d)], part_r.at[c, spot(d)])
+            unless(head, d == line - 1, lambda d=d: landed(got.at[c, spot(d)], part_r.at[c, spot(d)]))
             pooled = pooled + got[c, spot(d)]
         span = slice(c * width, (c + 1) * width)
         totals.append(base[:, span] + pooled * PICKS ** (-0.5) * small_rows[:, span])
@@ -143,8 +212,17 @@
     scale = lax.rsqrt(power + 1e-06)
     for c in range(CHUNKS):
         out[:, cols(c)] = totals[c] * scale
-    for copy in id_copies + tab_copies + [small_pair] + small_line + part_copies:
+    for copy in tab_copies + [small_pair] + list(small_line.values()):
         copy.wait_send()
+    for d, copy in id_copies.items():
+        unless(head, d == line - 1, copy.wait_send)
+    for d, copy in part_copies:
+        unless(tail, d == line - 1, copy.wait_send)
+
+    @pl.when(pusher)
+    def _():
+        for copy in raw_copies:
+            copy.wait_send()
 
 
 def solution(mesh):
@@ -169,8 +247,9 @@
                 pltpu.VMEM((1, examples), jnp.int32),
                 pltpu.VMEM((line, 2, held, feats), jnp.bfloat16),
                 pltpu.VMEM((1, examples), jnp.int32),
-                pltpu.VMEM((CHUNKS, line * examples, width), jnp.float32),
                 pltpu.VMEM((CHUNKS, line, examples, width), jnp.float32),
+                pltpu.VMEM((CHUNKS, line, examples, width), jnp.float32),
+                pltpu.VMEM((2, CHUNKS, rows, width), jnp.bfloat16),
                 dma((5,)),
                 dma((CHUNKS,)),
                 dma((line,)),
@@ -183,6 +262,10 @@
                 dma((line,)),
                 dma((CHUNKS, line)),
                 dma((CHUNKS, line)),
+                dma((CHUNKS,)),
+                dma((2, CHUNKS)),
+                pltpu.SemaphoreType.REGULAR,
+                pltpu.SemaphoreType.REGULAR((line,)),
             ],
             compiler_params=pltpu.CompilerParams(
                 collective_id=0, has_side_effects=True

time: 14.4 us -> 13.7 us (0.951)
  Pallas kernels: 13.6 us -> 12.9 us
    pallas_call x1, Pallas kernels: 13.6 us -> 12.9 us  [shards(): pl.pallas_call(functools.partial(kernel, n), out_shape=pltpu.VMEM((exampl...]
where the time goes in v3:
time: 13.7 us; the launch traced here: 13.6 us
  Pallas kernels  12.9 us (94%)
  local copies, waits for them, and re-layouts  0.62 us (5%)
    pallas_call x1, Pallas kernels, shards(): pl.pallas_call(functools.partial(kernel, n), out_shape=pltpu.VMEM((exampl...  12.9 us
    unnamed x1, local copies, waits for them, and re-layouts  0.62 us

profile of v3, /device:TPU:0, one launch (start us, length us, event | category | flops | bytes accessed | tf_op | source)
XLA Modules:
  0.0 13.6 jit_solution(14659574683814769232)
XLA Ops:
  0.0 12.9 %shard_map.64 = f32[32,256]{1,0:T(8,128)S(1)} custom-call(s32[2,32]{1,0:T(2,128)} %bitcast.3, bf16[256,256]{1,0:T(8,128)(2,1)} %tab_in.1, f32[32,256]{1,0:T(8,128)} %dense_in.1, s32[1,32]{1,0:T(1,128)} %bitcast.4, bf16[2,256]{1,0:T(2,128)(2,1)} %small_in.1, s32[1,32]{1,0:T(1,128)} %bitcast.5), custom_call_target="tpu_custom_call" | custom-call | tf_op jit(solution)/shard_map/pallas_call | solution.py:238
  12.9 0.6 %copy.8 = f32[32,256]{1,0:T(8,128)} copy(f32[32,256]{1,0:T(8,128)S(1)} %shard_map.64) | data formatting | bytes 65536

commit v4 on v3

--- a/solution.py
+++ b/solution.py
@@ -151,28 +151,26 @@
     for d in away:
         unless(head, d == line - 1, small_line[d].start)
     part_copies = []
-    for d in range(1, line):
-        unless(tail, d == line - 1, lambda d=d: landed(ids.at[spot(d)], ids_r.at[spot(d)]))
-        if d == line - 1:
-
-            @pl.when(head)
-            def _():
-                pl.semaphore_wait(here.at[spot(line - 1)], 1)
-
-        counts = counted(spot(d))
-        for c in range(CHUNKS):
-            if d == 1:
-                tab_copies[c].wait_recv()
-            part[c, d] = summed(counts, c)
+    counts = {}
+    for c in range(CHUNKS):
+        tab_copies[c].wait_recv()
+        for d in range(1, line):
+            if c == 0:
+                unless(tail, d == line - 1, lambda d=d: landed(ids.at[spot(d)], ids_r.at[spot(d)]))
+                counts[d] = counted(spot(d))
+                if d == line - 1:
+
+                    @pl.when(head)
+                    def _():
+                        pl.semaphore_wait(here.at[spot(line - 1)], 1)
+
+            part[c, d] = summed(counts[d], c)
             copy = remote(part.at[c, d], got.at[c, z], part_s.at[c, d], part_r.at[c, z], on_line(d))
             unless(tail, d == line - 1, copy.start)
             part_copies.append((d, copy))
     pl.when(head)(small_line[line - 1].start)
-    if line == 1:
-        for copy in tab_copies:
-            copy.wait_recv()
-    counts = counted(z)
-    kept = [summed(counts, c) for c in range(CHUNKS)]
+    own = counted(z)
+    kept = [summed(own, c) for c in range(CHUNKS)]
 
     for d in away:
         landed(small.at[spot(d)], sl_r.at[spot(d)])

time: 13.7 us -> 13.4 us (0.978)
  Pallas kernels: 12.9 us -> 12.6 us
    pallas_call x1, Pallas kernels: 12.9 us -> 12.6 us  [shards(): pl.pallas_call(functools.partial(kernel, n), out_shape=pltpu.VMEM((exampl...]
where the time goes in v4:
time: 13.4 us; the launch traced here: 13.2 us
  Pallas kernels  12.6 us (94%)
  local copies, waits for them, and re-layouts  0.62 us (5%)
    pallas_call x1, Pallas kernels, shards(): pl.pallas_call(functools.partial(kernel, n), out_shape=pltpu.VMEM((exampl...  12.6 us
    unnamed x1, local copies, waits for them, and re-layouts  0.62 us

profile of v4, /device:TPU:0, one launch (start us, length us, event | category | flops | bytes accessed | tf_op | source)
XLA Modules:
  0.0 13.2 jit_solution(6508040788372405467)
XLA Ops:
  0.0 12.6 %shard_map.64 = f32[32,256]{1,0:T(8,128)S(1)} custom-call(s32[2,32]{1,0:T(2,128)} %bitcast.3, bf16[256,256]{1,0:T(8,128)(2,1)} %tab_in.1, f32[32,256]{1,0:T(8,128)} %dense_in.1, s32[1,32]{1,0:T(1,128)} %bitcast.4, bf16[2,256]{1,0:T(2,128)(2,1)} %small_in.1, s32[1,32]{1,0:T(1,128)} %bitcast.5), custom_call_target="tpu_custom_call" | custom-call | tf_op jit(solution)/shard_map/pallas_call | solution.py:236
  12.6 0.6 %copy.8 = f32[32,256]{1,0:T(8,128)} copy(f32[32,256]{1,0:T(8,128)S(1)} %shard_map.64) | data formatting | bytes 65536
